TPU v7x, 512 devices: a whole 4x4x16 slice. The times are simulated.
512 devices in a mesh: rows: 128 (over y_lo, x, z), cols: 4 (over y_hi, core).
Axes of the slice: x: 4, y: 4 (y_hi: 2, y_lo: 2; y = y_hi * 2 + y_lo), z: 16, core: 2. Of those that a mesh axis runs over, the one named last changes fastest.
Arguments:
- grad_out: bfloat16 [512, 512, 192], P(('rows', 'cols')), may hold values from -6 to 6
- inputs: bfloat16 [1024, 1024, 192], P('rows', 'cols'), may hold values from -6 to 6
- weight: bfloat16 [3, 3, 192, 192], replicated, may hold values from -0.15625 to 0.15625
Outputs:
- input_grad: bfloat16 [1024, 1024, 192], P('rows', 'cols')
- filter_grad: float32 [3, 3, 192, 192], replicated
All inputs are finite; a program needn't handle non-finite values.
Results may differ from a plain program's by a relative error of at most 0.0028.
Values may be sent and summed in bfloat16 or wider, within the bound.
A program may use at most 64 MiB of HBM per device.

v0:
```python
import math

import jax
import jax.numpy as jnp
from jax import lax
from jax.sharding import Mesh
from jax.sharding import PartitionSpec as P

COLS = ("cols_0", "cols_1")
ROWS = ("rows_0", "rows_1", "rows_2")
ROWS_COLS = ("rows_0", "rows_1", "rows_2", "cols_0", "cols_1")


def shifted(x, axis, by):
    devices = lax.axis_size(axis)
    pairs = [(i, i + by) for i in range(devices) if 0 <= i + by < devices]
    return lax.ppermute(x, axis, pairs)


def rows_for(lines, devices):
    spare = -lines.shape[0] % devices
    if not spare:
        return lines
    return jnp.concatenate([lines, jnp.zeros((spare, *lines.shape[1:]), lines.dtype)])


def nested_sum(x, near, far):
    lines = x.reshape(-1, *x.shape[1:][-1:])
    padded = rows_for(lines, lax.axis_size(near))
    own = lax.psum_scatter(padded, near, scatter_dimension=0, tiled=True)
    own = lax.psum(own, far)
    whole = lax.all_gather(own, near, axis=0, tiled=True)
    return whole[: len(lines)].reshape(x.shape)


def tap_products(out_block, flat_weight):
    chans = flat_weight.shape[0]
    flat = out_block.reshape(-1, chans)
    products = jnp.dot(flat, flat_weight, preferred_element_type=jnp.float32)
    return products.reshape(out_block.shape[0], out_block.shape[1], 3, 3, chans)


def assemble(products, count_rows, count_cols):
    rows_even = products[:count_rows, :, 1]
    rows_odd = products[:count_rows, :, 2] + products[1 : count_rows + 1, :, 0]

    def columns(mixed):
        even = mixed[:, :count_cols, 1]
        odd = mixed[:, :count_cols, 2] + mixed[:, 1 : count_cols + 1, 0]
        return jnp.stack([even, odd], axis=2)

    placed = jnp.stack([columns(rows_even), columns(rows_odd)], axis=1)
    return placed.reshape(2 * count_rows, 2 * count_cols, products.shape[-1])


def filter_terms(input_band, out_band, row_taps):
    count_rows, count_cols, chans = out_band.shape
    split = input_band.reshape(count_rows + 1, 2, count_cols + 1, 2, chans)
    offsets = ((0, 0), (0, 1), (1, 0))
    pieces = []
    for row_tap in row_taps:
        start_row, parity_row = offsets[row_tap]
        for col_tap in range(3):
            start_col, parity_col = offsets[col_tap]
            pieces.append(
                split[
                    start_row : start_row + count_rows,
                    parity_row,
                    start_col : start_col + count_cols,
                    parity_col,
                ]
            )
    stacked = jnp.stack(pieces, axis=2).reshape(count_rows * count_cols, len(pieces) * chans)
    flat_out = out_band.reshape(count_rows * count_cols, chans)
    return lax.dot_general(
        stacked, flat_out, (((0,), (0,)), ((), ())), preferred_element_type=jnp.float32
    )


def per_device(grad_out, inputs, weight):
    chans = weight.shape[2]
    rows_local, cols_local = (inputs.shape[0], inputs.shape[1])
    half_rows, half_cols = (rows_local // 2, cols_local // 2)
    out_grad = lax.all_to_all(grad_out, COLS, split_axis=1, concat_axis=0, tiled=True)
    flat_weight = jnp.transpose(weight, (3, 0, 1, 2)).reshape(chans, 9 * chans)
    above = shifted(inputs[-1:], ROWS, 1)
    with_above = jnp.concatenate([above, inputs], axis=0)
    left = shifted(with_above[:, -1:], COLS, 1)
    input_band = jnp.pad(jnp.concatenate([left, with_above], axis=1), ((0, 1), (0, 1), (0, 0)))
    positions = half_rows * lax.axis_size(ROWS) * (half_cols * lax.axis_size(COLS))
    scale = 1.0 / math.sqrt(positions)
    terms = filter_terms(input_band, out_grad, (0, 1, 2))
    summed = nested_sum(terms, "cols_1", ("rows_0", "rows_1", "rows_2", "cols_0"))
    filter_grad = summed.reshape(3, 3, chans, chans) * scale
    below = shifted(out_grad[:1], ROWS, -1)
    with_below = jnp.concatenate([out_grad, below], axis=0)
    right = shifted(with_below[:, :1], COLS, -1)
    out_block = jnp.concatenate([with_below, right], axis=1)
    input_grad = assemble(tap_products(out_block, flat_weight), half_rows, half_cols)
    return (input_grad.astype(jnp.bfloat16), filter_grad)


def solution(mesh):
    split = Mesh(
        mesh.devices.reshape(2, 4, 16, 2, 2), ("rows_0", "rows_1", "rows_2", "cols_0", "cols_1")
    )
    return jax.shard_map(
        per_device,
        mesh=split,
        in_specs=(P(ROWS_COLS, None, None), P(ROWS, COLS, None), P()),
        out_specs=(P(ROWS, COLS, None), P()),
        check_vma=False,
    )
```

profile of v0, /device:TPU:1, one launch (start us, length us, event | category | flops | bytes accessed | tf_op | source)
XLA Modules:
  0.0 525.2 jit_solution(7369286087531023577)
XLA Ops:
  8.2 4.4 collective-permute-start.2
  12.6 1.6 collective-permute-done.2
  14.2 1.2 constant_dynamic-update-slice_fusion
  15.6 6.2 %collective-permute-start.3 = (bf16[9,1,192]{1,2,0:T(8,128)(2,1)S(1)}, bf16[9,1,192]{1,2,0:T(8,128)(2,1)S(1)}, u32[]{:S(2)}, u32[]{:S(2)}) collective-permute-start(bf16[9,1,192]{1,2,0:T(8,128)(2,1)S(1)} %slice.101), channel_id=1, source_target_pairs={{0,1},{1,2},{2,3},{4,5},{5,6},{6,7},{8,9},{9,10},{10,11},{12,13},{... | collective-permute-start | bytes 10376 | tf_op jit(solution)/shard_map/ppermute | solution.py:17
  22.8 2.3 reduce
  26.1 4.0 all-to-all-start
  30.8 2.0 copy.231
  32.8 1.3 pad.4.clone
  34.1 3.1 reshape.33
  37.2 4.4 fusion.14
  41.7 1.2 copy.211
  43.6 1.9 copy.212
  45.5 1.8 copy.213
  47.4 1.8 copy.214
  49.2 1.2 copy.215
  51.9 1.6 bitcast_dynamic-update-slice_fusion.7
  53.6 1.6 bitcast_dynamic-update-slice_fusion.6
  59.5 2.8 copy.220
  62.3 1.3 reshape.47
  63.9 1.9 fusion
  65.9 24.6 %reduce-scatter.4.cloned.1.call-done = f32[864,192]{1,0:T(8,128)} async-done(((f32[1728,192]{1,0:T(8,128)}), f32[864,192]{1,0:T(8,128)}) %reduce-scatter.4.cloned.1.call-update) | async-done | bytes 663568
  90.5 2.3 copy.227
  93.0 1.3 collective-permute-start
  94.3 4.4 collective-permute-done
  98.8 2.7 collective-permute-start.1
  101.5 385.6 %all-reduce.3.cloned.1.call-done = f32[864,192]{0,1:T(8,128)} async-done(((f32[864,192]{0,1:T(8,128)}), f32[864,192]{0,1:T(8,128)}) %all-reduce.3.cloned.1.call-update) | async-done | bytes 663568 | tf_op jit(solution)/shard_map/psum | solution.py:31
  489.1 1.1 copy.209
  490.2 1.0 convert_element_type.6
  491.2 1.3 copy.223
  492.5 22.9 %all-gather.3.cloned.1.call-done = f32[2,864,192]{1,2,0:T(8,128)} async-done(((f32[1,864,192]{1,2,0:T(8,128)}), f32[2,864,192]{1,2,0:T(8,128)}) %all-gather.3.cloned.1.call-update) | async-done | bytes 1327120 | tf_op jit(solution)/shard_map/all_gather | solution.py:32
  515.4 1.9 copy.222
  517.3 1.3 broadcast_multiply_fusion
  (50 shorter events, 12.9 us)
Async XLA Ops:
  7.2 479.9 %copy-start = (bf16[3,3,192,192]{3,2,1,0:T(8,128)(2,1)S(1)}, bf16[3,3,192,192]{3,2,1,0:T(8,128)(2,1)}, u32[]{:S(2)}) copy-start(bf16[3,3,192,192]{3,2,1,0:T(8,128)(2,1)} %param.5) | copy-start | bytes 1990660
  7.2 14.6 %copy-start.4 = (bf16[1,512,192]{1,2,0:T(8,128)(2,1)S(1)}, bf16[1,512,192]{1,2,0:T(8,128)(2,1)}, u32[]{:S(2)}) copy-start(bf16[1,512,192]{1,2,0:T(8,128)(2,1)} %param.3) | copy-start | bytes 589828
  8.2 6.0 %collective-permute-start.2 = (bf16[1,256,192]{1,2,0:T(8,128)(2,1)S(1)}, bf16[1,256,192]{1,2,0:T(8,128)(2,1)S(1)}, u32[]{:S(2)}, u32[]{:S(2)}) collective-permute-start(bf16[1,256,192]{1,2,0:T(8,128)(2,1)S(1)} %slice.80), channel_id=1, source_target_pairs={{0,4},{4,8},{8,12},{12,16},{16,20},{20,24},{24,28},{28,32},{32,36}... | collective-permute-start | bytes 294920 | tf_op jit(solution)/shard_map/ppermute | solution.py:17
  15.6 14.6 %collective-permute-start.3 = (bf16[9,1,192]{1,2,0:T(8,128)(2,1)S(1)}, bf16[9,1,192]{1,2,0:T(8,128)(2,1)S(1)}, u32[]{:S(2)}, u32[]{:S(2)}) collective-permute-start(bf16[9,1,192]{1,2,0:T(8,128)(2,1)S(1)} %slice.101), channel_id=1, source_target_pairs={{0,1},{1,2},{2,3},{4,5},{5,6},{6,7},{8,9},{9,10},{10,11},{12,13},{... | collective-permute-start | bytes 10376 | tf_op jit(solution)/shard_map/ppermute | solution.py:17
  26.1 36.2 %all-to-all-start = ((bf16[4,2,12288]{2,1,0:T(2,128)(2,1)}), bf16[4,2,12288]{2,1,0:T(2,128)(2,1)}, u32[]{:S(2)}, u32[]{:S(2)}) async-start(bf16[4,2,12288]{2,1,0:T(2,128)(2,1)} %reshape.46), calls=%async_computation | async-start | bytes 393216 | tf_op jit(solution)/shard_map/all_to_all | solution.py:84
  30.1 60.4 %reduce-scatter.4.cloned.1.call-start = ((), (), s32[]{:S(2)}) async-start(), calls=%async_computation.4 | async-start | bytes 2654208
  42.9 7.6 %copy-start.2 = (bf16[4,1,128,1,192]{4,3,2,1,0:T(2,128)(2,1)S(1)}, bf16[4,1,128,1,192]{4,3,2,1,0:T(2,128)(2,1)}, u32[]{:S(2)}) copy-start(bf16[4,1,128,1,192]{4,3,2,1,0:T(2,128)(2,1)} %get-tuple-element.29) | copy-start | bytes 589828
  43.6 7.2 %copy-start.1 = (bf16[4,1,128,1,192]{4,3,2,1,0:T(2,128)(2,1)S(1)}, bf16[4,1,128,1,192]{4,3,2,1,0:T(2,128)(2,1)}, u32[]{:S(2)}) copy-start(bf16[4,1,128,1,192]{4,3,2,1,0:T(2,128)(2,1)} %get-tuple-element.28) | copy-start | bytes 589828
  50.8 4.4 copy-start.3
  65.8 421.3 %all-reduce.3.cloned.1.call-start = ((), (), s32[]{:S(2)}) async-start(), calls=%async_computation.2 | async-start | bytes 1376256 | tf_op jit(solution)/shard_map/psum | solution.py:31
  92.8 422.7 %all-gather.3.cloned.1.call-start = ((), (), s32[]{:S(2)}) async-start(), calls=%async_computation.3 | async-start | bytes 2064384 | tf_op jit(solution)/shard_map/all_gather | solution.py:32
  93.0 5.8 %collective-permute-start = (bf16[1,128,192]{2,1,0:T(8,128)(2,1)S(1)}, bf16[1,128,192]{2,1,0:T(8,128)(2,1)S(1)}, u32[]{:S(2)}, u32[]{:S(2)}) collective-permute-start(bf16[1,128,192]{2,1,0:T(8,128)(2,1)S(1)} %copy.229), channel_id=1, source_target_pairs={{4,0},{8,4},{12,8},{16,12},{20,16},{24,20},{28,24},{32,28},{36,32}... | collective-permute-start | bytes 147464 | tf_op jit(solution)/shard_map/ppermute | solution.py:17
  98.8 388.3 %collective-permute-start.1 = (bf16[5,1,192]{2,1,0:T(2,128)(2,1)S(1)}, bf16[5,1,192]{2,1,0:T(2,128)(2,1)S(1)}, u32[]{:S(2)}, u32[]{:S(2)}) collective-permute-start(bf16[5,1,192]{2,1,0:T(2,128)(2,1)S(1)} %pad_maximum_fusion.2), channel_id=1, source_target_pairs={{1,0},{2,1},{3,2},{5,4},{6,5},{7,6},{9,8},{10,9},{11,10},{13,12},{... | collective-permute-start | bytes 5768 | tf_op jit(solution)/shard_map/ppermute | solution.py:17
Sparse Core Ops, SparseCore 0:
  65.9 24.4 reduce-scatter.3
  96.4 390.6 all-reduce.2
  489.2 26.2 all-gather.2
where the time goes:
time: 526 us; the launch traced here: 525 us
  waiting for transfers between devices  439 us (83%)
  local copies, waits for them, and re-layouts  45.1 us (9%)
  starting transfers between devices  18.7 us (4%)
  between operations  14.1 us (3%)
    psum x1, waiting for transfers between devices, nested_sum(): own = lax.psum(own, far)  386 us
    unnamed x4, waiting for transfers between devices  24.6 us
    all_gather x1, waiting for transfers between devices, nested_sum(): whole = lax.all_gather(own, near, axis=0, tiled=True)  22.9 us
    unnamed x28, local copies, waits for them, and re-layouts  16.4 us
    ppermute x4, starting transfers between devices, shifted(): return lax.ppermute(x, axis, pairs)  14.6 us
    slice x10, local copies, waits for them, and re-layouts, filter_terms(): split[start_row:start_row + count_rows, parity_row, start_col:start_col +...  13.9 us
  transfers between devices with their start and end apart: 8, of which 5 were waited for; matrix products, arithmetic and copies ran while one was open for 8% of the time, Pallas kernels for 0%

commit v1 on v0

v1 whole, which is shorter than its diff:
```python
import functools

import jax
import jax.numpy as jnp
from jax import lax
from jax.experimental import pallas as pl
from jax.experimental.pallas import tpu as pltpu
from jax.sharding import Mesh
from jax.sharding import PartitionSpec as P

MESH = pl.DeviceIdType.MESH
YLO, X, Z, YHI, CORE = "rows_0", "rows_1", "rows_2", "cols_0", "cols_1"
COLS = (YHI, CORE)
ROWS = (YLO, X, Z)
F32, BF16 = jnp.float32, jnp.bfloat16
C = 192
TAP_ROWS = C + C // 2
HALF = 9 * TAP_ROWS // 2


def dot_nn(a, b):
    return lax.dot_general(a, b, (((1,), (0,)), ((), ())), preferred_element_type=F32)


def dot_nt(a, b):
    return lax.dot_general(a, b, (((1,), (1,)), ((), ())), preferred_element_type=F32)


def iota(shape, dim):
    return lax.broadcasted_iota(jnp.int32, shape, dim)


def kernel(sizes, g_hbm, x_hbm, w_hbm, ig_hbm, fg_hbm, gsend, gcat, gshift, xin, w, xd, ig2, igo, terms, dbuf,
           sbuf, rbuf, acc, zbuf, zfar, zown, fin, agbuf, fgo,
           load_sem, gs_sem, gr_sem, ds_sem, dr_sem, xs_sem, xr_sem, ns_sem, nr_sem, fs_sem, fr_sem,
           as_sem, ar_sem, os_sem, or_sem, ps_sem, pr_sem, out_sem):
    nyl, nx, nz, nyh, nzl, chunk, scale = sizes
    planes = nx * nyl * nyh
    nzh = nz // nzl
    piece = chunk // nzl
    ny = nyl * nyh
    rows = nyl * nx * nz
    yl, x, z, yh, core = (lax.axis_index(a) for a in (YLO, X, Z, YHI, CORE))
    row = (yl * nx + x) * nz + z
    col = yh * 2 + core
    y = yh * nyl + yl
    me = x * ny + y
    zh, zl = z // nzl, z % nzl

    load_g = pltpu.make_async_copy(g_hbm, gsend.at[0:C], load_sem.at[0])
    load_x = pltpu.make_async_copy(x_hbm, xin, load_sem.at[1])
    load_w = pltpu.make_async_copy(w_hbm, w, load_sem.at[2])
    load_g.start()
    load_x.start()
    load_w.start()

    def at_row(r):
        return {YLO: r // (nx * nz), X: (r // nz) % nx, Z: r % nz}

    def at_col(c):
        return {YHI: c // 2, CORE: c % 2}

    def at_plane(dx, dy):
        px, py = (x + dx) % nx, (y + dy) % ny
        return px * ny + py, {X: px, YHI: py // nyl, YLO: py % nyl}

    offsets = [(dx, dy) for dx in range(nx) for dy in range(ny) if (dx, dy) != (0, 0)]
    offsets.sort(key=lambda o: -(min(o[0], nx - o[0]) + min(o[1], ny - o[1])))

    barrier = pltpu.get_barrier_semaphore()

    def greet(where):
        pl.semaphore_signal(barrier, inc=1, device_id=where, device_id_type=MESH)

    for d in range(1, nzh):
        greet({Z: ((zh + d) % nzh) * nzl + zl})
    for d in range(1, nzl):
        greet({Z: zh * nzl + (zl + d) % nzl})
    for dx, dy in offsets:
        greet(at_plane(dx, dy)[1])
    greet({CORE: 1 - core})
    greet({CORE: 1 - core, YHI: 1 - yh})

    @pl.when(row < rows - 1)
    def _():
        greet(at_row(row + 1) | at_col(0))

    met = (nzh - 1) + (nzl - 1) + len(offsets) + 2

    load_g.wait()
    blocks = 4
    width = gsend.shape[1]
    sel_row, sel_col = iota((16, width), 0), iota((16, width), 1)
    for c in range(blocks - 1):
        hit = sel_col == 128 * (c + 1)
        first = jnp.where(hit & (sel_row == 0), 1.0, 0.0).astype(BF16)
        second = jnp.where(hit & (sel_row == 1), 1.0, 0.0).astype(BF16)
        tile = dot_nt(first, gsend[0:128, :]) + dot_nt(second, gsend[64:192, :])
        gsend[C : C + 16, 128 * c : 128 * c + 128] = tile.astype(BF16)
    gsend[C : C + 16, 128 * (blocks - 1) :] = jnp.zeros((16, 128), BF16)
    own = pl.multiple_of(col * 128, 128)
    gcat[:, pl.ds(own, 128)] = gsend[:, pl.ds(own, 128)]

    @pl.when(row == rows - 1)
    def _():
        gcat[:, 512:640] = jnp.zeros((C + 16, 128), BF16)

    load_x.wait()
    r256, c256 = iota((256, 256), 0), iota((256, 256), 1)
    part = jnp.where(r256 == 2 * (c256 % 128) + c256 // 128, 1.0, 0.0).astype(BF16)
    join = jnp.where(c256 == 2 * (r256 % 128) + r256 // 128, 1.0, 0.0).astype(BF16)
    for p in range(8):
        both = dot_nn(xin[p], part).astype(BF16)
        lanes = slice(128 * (p // 2), 128 * (p // 2) + 128)
        xd[p % 2, 0, :, lanes] = both[:, 0:128]
        xd[p % 2, 1, :, lanes] = both[:, 128:256]

    @pl.when((col == 0) & (row > 0))
    def _():
        pl.semaphore_wait(barrier, met + 4)

    @pl.when((col != 0) | (row == 0))
    def _():
        pl.semaphore_wait(barrier, met)

    def g_copy(c, slot, where, sem):
        return pltpu.make_async_remote_copy(
            src_ref=gsend.at[:, pl.ds(pl.multiple_of(c * 128, 128), 128)],
            dst_ref=gcat.at[:, pl.ds(pl.multiple_of(slot * 128, 128), 128)],
            send_sem=gs_sem.at[sem], recv_sem=gr_sem.at[slot], device_id=where, device_id_type=MESH)

    peers = [(col + d) % 4 for d in (2, 3, 1)]
    g_sent = [g_copy(c, col, at_col(c), n) for n, c in enumerate(peers)]
    for copy in g_sent:
        copy.start()
    upward = [g_copy(c, 4, at_row(row - 1) | at_col(c), 3 + c) for c in range(4)]

    @pl.when((col == 0) & (row > 0))
    def _():
        for copy in upward:
            copy.start()

    for d in (1, 2, 3):
        g_copy(0, (col + d) % 4, at_col(0), 0).wait_recv()

    @pl.when(row < rows - 1)
    def _():
        g_copy(0, 4, at_col(0), 0).wait_recv()

    r128, c128 = iota((128, 128), 0), iota((128, 128), 1)
    shift = jnp.where(r128 == c128 + 1, 1.0, 0.0).astype(BF16)
    eye = jnp.where(r128 == c128, 1.0, 0.0).astype(BF16)
    for i in range(5):
        lanes = slice(128 * i, 128 * i + 128)
        moved = dot_nn(gcat[0:C, lanes], shift)
        tile = gcat[C : C + 16, lanes].astype(F32)
        edge0 = jnp.where(r128 == 127, tile[0:1, :], 0.0).astype(BF16)
        edge1 = jnp.where(r128 == 127, tile[1:2, :], 0.0).astype(BF16)
        gshift[0:128, lanes] = (moved[0:128] + dot_nt(eye, edge0)).astype(BF16)
        gshift[128:192, lanes] = (moved[128:192] + dot_nt(eye, edge1)[64:128]).astype(BF16)

    def grad(down, right):
        ref = gshift if right else gcat
        return ref, slice(128 * down, 128 * down + 512)

    taps = {0: (1, 1), 1: (0, 0), 2: (1, 0)}
    low = iota((C // 2, 128), 1) < 64
    for t in range(9):
        (row_par, down), (col_par, right) = taps[t // 3], taps[t % 3]
        ref, lanes = grad(down, right)
        lhs = xd[row_par, col_par]
        main = dot_nt(lhs, ref[0:128, lanes])
        rest = dot_nt(lhs, ref[64:192, lanes])
        rest = jnp.where(low, pltpu.roll(rest[0 : C // 2], 64, 1), rest[C // 2 : C])
        start = TAP_ROWS * t
        for begin, values in ((start, main), (start + C, rest)):
            count = values.shape[0]
            cut = min(max(HALF - begin, 0), count)
            if cut > 0:
                terms[0, begin : begin + cut] = values[0:cut]
            if cut < count:
                terms[1, begin + cut - HALF : begin + count - HALF] = values[cut:]
    spare = planes * chunk - HALF
    if spare:
        for h in range(2):
            terms[h, HALF:] = jnp.zeros((spare, 128), F32)

    pair = pltpu.make_async_remote_copy(
        src_ref=terms.at[1 - core], dst_ref=dbuf, send_sem=ds_sem, recv_sem=dr_sem,
        device_id={CORE: 1 - core}, device_id_type=MESH)
    pair.start()
    pair.wait_recv()

    def plane_copy(n, source, slot, where):
        return pltpu.make_async_remote_copy(
            src_ref=sbuf.at[source], dst_ref=rbuf.at[slot], send_sem=xs_sem.at[n], recv_sem=xr_sem.at[slot],
            device_id=where, device_id_type=MESH)

    plane_sent = []
    for n, (dx, dy) in enumerate(offsets):
        q, where = at_plane(dx, dy)
        at = pl.ds(pl.multiple_of(q * chunk, chunk), chunk)
        sbuf[q] = (terms[core, at, :] + dbuf[at, :]).astype(BF16)
        copy = plane_copy(n, q, me, where)
        copy.start()
        plane_sent.append(copy)
    at = pl.ds(pl.multiple_of(me * chunk, chunk), chunk)
    acc[...] = terms[core, at, :] + dbuf[at, :]

    load_w.wait()

    def tap(a, b):
        return w[3 * a + b]

    def apply(pairs):
        total = None
        for (a, b), (down, right) in pairs:
            ref, lanes = grad(down, right)
            one = dot_nn(tap(a, b), ref[0:C, lanes])
            total = one if total is None else total + one
        return total.astype(BF16)

    plan = {
        (0, 0): [((1, 1), (0, 0))],
        (0, 1): [((1, 2), (0, 0)), ((1, 0), (0, 1))],
        (1, 0): [((2, 1), (0, 0)), ((0, 1), (1, 0))],
        (1, 1): [((2, 2), (0, 0)), ((2, 0), (0, 1)), ((0, 2), (1, 0)), ((0, 0), (1, 1))],
    }
    for (row_par, col_par), pairs in plan.items():
        placed = apply(pairs)
        for i in range(4):
            ig2[row_par, i, :, 128 * col_par : 128 * col_par + 128] = placed[:, 128 * i : 128 * i + 128]
    for p in range(8):
        igo[p] = dot_nn(ig2[p % 2, p // 2], join).astype(BF16)
    store_ig = pltpu.make_async_copy(igo, ig_hbm, out_sem.at[0])
    store_ig.start()

    total = acc[...]
    for dx, dy in reversed(offsets):
        q, where = at_plane(dx, dy)
        plane_copy(0, q, q, where).wait_recv()
        total += rbuf[q].astype(F32)
    acc[...] = total

    def near_copy(n, k, slot, where):
        return pltpu.make_async_remote_copy(
            src_ref=acc.at[pl.ds(pl.multiple_of(k * piece, 8), piece)], dst_ref=zbuf.at[slot],
            send_sem=ns_sem.at[n], recv_sem=nr_sem.at[slot], device_id={Z: where}, device_id_type=MESH)

    near_sent = []
    for d in range(1, nzl):
        k = (zl + d) % nzl
        copy = near_copy(d - 1, k, zl, zh * nzl + k)
        copy.start()
        near_sent.append(copy)
    total = acc[pl.ds(pl.multiple_of(zl * piece, 8), piece)]
    for d in range(1, nzl):
        k = (zl + d) % nzl
        near_copy(0, k, k, z).wait_recv()
        total += zbuf[k]
    zown[...] = total
    zfar[zh] = total

    def far_copy(n, slot, where):
        return pltpu.make_async_remote_copy(
            src_ref=zown, dst_ref=zfar.at[slot], send_sem=fs_sem.at[n], recv_sem=fr_sem.at[slot],
            device_id={Z: where}, device_id_type=MESH)

    far_sent = []
    for n, d in enumerate(sorted(range(1, nzh), key=lambda d: -min(d, nzh - d))):
        copy = far_copy(n, zh, ((zh + d) % nzh) * nzl + zl)
        copy.start()
        far_sent.append(copy)
    for d in range(1, nzh):
        far_copy(0, (zh + d) % nzh, z).wait_recv()
    total = zfar[0]
    for k in range(1, nzh):
        total += zfar[k]
    mine = pl.ds(pl.multiple_of(zl * piece, 8), piece)
    fin[mine] = total

    def gather_copy(n, k, where):
        part_of = pl.ds(pl.multiple_of(k * piece, 8), piece)
        return pltpu.make_async_remote_copy(
            src_ref=fin.at[part_of], dst_ref=fin.at[part_of], send_sem=as_sem.at[n], recv_sem=ar_sem.at[k],
            device_id={Z: where}, device_id_type=MESH)

    gather_sent = []
    for d in range(1, nzl):
        copy = gather_copy(d - 1, zl, zh * nzl + (zl + d) % nzl)
        copy.start()
        gather_sent.append(copy)
    for d in range(1, nzl):
        gather_copy(0, (zl + d) % nzl, z).wait_recv()

    def ag_at(h, q):
        return agbuf.at[h, pl.ds(pl.multiple_of(q * chunk, chunk), chunk)]

    def spread_copy(n, q, where):
        return pltpu.make_async_remote_copy(
            src_ref=ag_at(core, q), dst_ref=ag_at(core, q), send_sem=os_sem.at[n], recv_sem=or_sem.at[q],
            device_id=where, device_id_type=MESH)

    def pass_copy(q, half):
        return pltpu.make_async_remote_copy(
            src_ref=ag_at(half, q), dst_ref=ag_at(half, q), send_sem=ps_sem.at[q], recv_sem=pr_sem.at[q],
            device_id={CORE: 1 - core}, device_id_type=MESH)

    agbuf[core, pl.ds(pl.multiple_of(me * chunk, chunk), chunk)] = fin[...].astype(BF16)
    spread_sent = []
    for n, (dx, dy) in enumerate(offsets):
        copy = spread_copy(n, me, at_plane(dx, dy)[1])
        copy.start()
        spread_sent.append(copy)
    pass_sent = [pass_copy(me, core)]
    pass_sent[0].start()
    for dx, dy in reversed(offsets):
        q = at_plane(dx, dy)[0]
        spread_copy(0, q, {}).wait_recv()
        copy = pass_copy(q, core)
        copy.start()
        pass_sent.append(copy)
    for q in range(planes):
        pass_copy(q, 1 - core).wait_recv()

    def packed(begin, count):
        cut = min(max(HALF - begin, 0), count)
        parts = []
        if cut > 0:
            parts.append(agbuf[0, begin : begin + cut])
        if cut < count:
            parts.append(agbuf[1, begin + cut - HALF : begin + count - HALF])
        values = parts[0] if len(parts) == 1 else jnp.concatenate(parts, axis=0)
        return values.astype(F32) * scale

    for t in range(9):
        start = TAP_ROWS * t
        fgo[t, :, 0:128] = packed(start, C)
        rest = packed(start + C, C // 2)
        fgo[t, 0 : C // 2, 128:C] = rest[:, 0:64]
        fgo[t, C // 2 : C, 128:C] = pltpu.roll(rest, 64, 1)[:, 0:64]
    store_fg = pltpu.make_async_copy(fgo, fg_hbm, out_sem.at[1])
    store_fg.start()

    for copy in g_sent + [pair] + plane_sent + near_sent + far_sent + gather_sent + spread_sent + pass_sent:
        copy.wait_send()

    @pl.when((col == 0) & (row > 0))
    def _():
        for copy in upward:
            copy.wait_send()

    store_ig.wait()
    store_fg.wait()


def near_size(nz):
    return 4 if nz % 4 == 0 and nz > 4 else max(nz // 2, 1)


def per_device(scale, grad_out, inputs, weight):
    nyl, nx, nz, nyh = (lax.axis_size(a) for a in (YLO, X, Z, YHI))
    planes = nx * nyl * nyh
    nzl = near_size(nz)
    chunk = -(-HALF // planes)
    chunk = -(-chunk // 96) * 96
    g = jnp.transpose(grad_out, (0, 2, 1)).reshape(C, grad_out.shape[1])
    xt = jnp.transpose(inputs, (0, 2, 1))
    wt = weight.reshape(9, C, C)
    sizes = (nyl, nx, nz, nyh, nzl, chunk, scale)
    dma = pltpu.SemaphoreType.DMA
    hbm = pl.BlockSpec(memory_space=pl.ANY)
    n = planes - 1
    nzh = nz // nzl
    piece = chunk // nzl
    ig, fg = pl.pallas_call(
        functools.partial(kernel, sizes),
        out_shape=(
            jax.ShapeDtypeStruct(xt.shape, BF16),
            jax.ShapeDtypeStruct((9, C, C), F32),
        ),
        in_specs=[hbm] * 3,
        out_specs=(hbm, hbm),
        scratch_shapes=[
            pltpu.VMEM((C + 16, 512), BF16),
            pltpu.VMEM((C + 16, 640), BF16),
            pltpu.VMEM((C, 640), BF16),
            pltpu.VMEM(xt.shape, BF16),
            pltpu.VMEM((9, C, C), BF16),
            pltpu.VMEM((2, 2, C, 512), BF16),
            pltpu.VMEM((2, 4, C, 256), BF16),
            pltpu.VMEM(xt.shape, BF16),
            pltpu.VMEM((2, planes * chunk, 128), F32),
            pltpu.VMEM((planes * chunk, 128), F32),
            pltpu.VMEM((planes, chunk, 128), BF16),
            pltpu.VMEM((planes, chunk, 128), BF16),
            pltpu.VMEM((chunk, 128), F32),
            pltpu.VMEM((nzl, piece, 128), F32),
            pltpu.VMEM((nzh, piece, 128), F32),
            pltpu.VMEM((piece, 128), F32),
            pltpu.VMEM((chunk, 128), F32),
            pltpu.VMEM((2, planes * chunk, 128), BF16),
            pltpu.VMEM((9, C, C), F32),
            dma((3,)), dma((7,)), dma((5,)), dma, dma, dma((n,)), dma((planes,)),
            dma((nzl,)), dma((nzl,)), dma((nzh,)), dma((nzh,)), dma((nzl,)), dma((nzl,)),
            dma((n,)), dma((planes,)), dma((planes,)), dma((planes,)), dma((2,)),
        ],
        compiler_params=pltpu.CompilerParams(
            collective_id=0, has_side_effects=True, vmem_limit_bytes=48 * 1024 * 1024
        ),
    )(g, xt, wt)
    return jnp.transpose(ig, (0, 2, 1)), fg.reshape(3, 3, C, C)


def solution(mesh):
    split = Mesh(mesh.devices.reshape(2, 4, 16, 2, 2), ROWS + COLS)
    positions = (4 * mesh.shape["rows"]) * (128 * mesh.shape["cols"])
    return jax.shard_map(
        functools.partial(per_device, positions ** -0.5),
        mesh=split,
        in_specs=(P(ROWS + COLS, None, None), P(ROWS, COLS, None), P()),
        out_specs=(P(ROWS, COLS, None), P()),
        check_vma=False,
    )
```

time: 526 us -> 62.5 us (0.12)
  waiting for transfers between devices: 439 us -> 0 us
  Pallas kernels: 0 us -> 56.3 us
  local copies, waits for them, and re-layouts: 45.1 us -> 5.31 us
  starting transfers between devices: 18.7 us -> 0 us
  between operations: 14.1 us -> 0.65 us
    psum x1 -> x0, waiting for transfers between devices: 386 us -> none  [nested_sum(): own = lax.psum(own, far)]
    pallas_call x0 -> x1, Pallas kernels: none -> 56.3 us  [per_device(): pl.pallas_call(functools.partial(kernel, sizes), out_shape=(jax.ShapeDtyp...]
    unnamed x4 -> x0, waiting for transfers between devices: 24.6 us -> none
    all_gather x1 -> x0, waiting for transfers between devices: 22.9 us -> none  [nested_sum(): whole = lax.all_gather(own, near, axis=0, tiled=True)]
    slice x15 -> x0, local copies, waits for them, and re-layouts: 15.3 us -> none  [the longest x10 13.9 us: filter_terms(): split[start_row:start_row + count_rows, parity_row, start_col:start_col +...]
    ppermute x4 -> x0, starting transfers between devices: 14.6 us -> none  [shifted(): return lax.ppermute(x, axis, pairs)]
    unnamed x28 -> x8, local copies, waits for them, and re-layouts: 16.4 us -> 5.31 us
    ppermute x4 -> x0, waiting for transfers between devices: 6.06 us -> none  [shifted(): return lax.ppermute(x, axis, pairs)]
  transfers between devices with their start and end apart: 8 -> 0, of which waited for: 5 -> 0; matrix products, arithmetic and copies ran while one was open for 8% -> 0% of each run, Pallas kernels for 0% -> 0%
where the time goes in v1:
time: 62.5 us; the launch traced here: 62.2 us
  Pallas kernels  56.3 us (90%)
  local copies, waits for them, and re-layouts  5.31 us (8%)
  between operations  0.65 us (1%)
    pallas_call x1, Pallas kernels, per_device(): pl.pallas_call(functools.partial(kernel, sizes), out_shape=(jax.ShapeDtyp...  56.3 us
    unnamed x8, local copies, waits for them, and re-layouts  5.31 us

profile of v1, /device:TPU:1, one launch (start us, length us, event | category | flops | bytes accessed | tf_op | source)
XLA Modules:
  0.0 62.2 jit_solution(11302944361805856000)
XLA Ops:
  0.6 0.0 copy-start
  0.6 1.2 %copy-done = bf16[3,3,192,192]{3,2,1,0:T(8,128)(2,1)S(1)} copy-done((bf16[3,3,192,192]{3,2,1,0:T(8,128)(2,1)S(1)}, bf16[3,3,192,192]{3,2,1,0:T(8,128)(2,1)}, u32[]{:S(2)}) %copy-start) | copy-done | bytes 663576
  1.8 0.0 copy-start.1
  1.8 1.1 %copy-done.1 = bf16[8,256,192]{1,2,0:T(8,128)(2,1)S(1)} copy-done((bf16[8,256,192]{1,2,0:T(8,128)(2,1)S(1)}, bf16[8,256,192]{1,2,0:T(8,128)(2,1)}, u32[]{:S(2)}) %copy-start.1) | copy-done | bytes 786456
  2.9 0.0 copy-start.2
  2.9 0.9 %copy-done.2 = bf16[1,512,192]{1,2,0:T(8,128)(2,1)S(1)} copy-done((bf16[1,512,192]{1,2,0:T(8,128)(2,1)S(1)}, bf16[1,512,192]{1,2,0:T(8,128)(2,1)}, u32[]{:S(2)}) %copy-start.2) | copy-done | bytes 196632
  3.9 56.3 %shard_map.50 = (bf16[8,192,256]{2,1,0:T(8,128)(2,1)S(1)}, f32[9,192,192]{2,1,0:T(8,128)S(1)}) custom-call(bf16[192,512]{1,0:T(8,128)(2,1)S(1)} %bitcast.11, bf16[8,192,256]{2,1,0:T(8,128)(2,1)S(1)} %bitcast.9, bf16[9,192,192]{2,1,0:T(8,128)(2,1)S(1)} %bitcast.8), custom_call_target="tpu_custom_call" | custom-call | tf_op jit(solution)/shard_map/pallas_call | solution.py:376
  60.1 0.9 %copy.7 = bf16[8,256,192]{1,2,0:T(8,128)(2,1)} copy(bf16[8,256,192]{1,2,0:T(8,128)(2,1)S(1)} %bitcast.10) | data formatting | bytes 1572864
  61.0 1.2 %copy.8 = f32[3,3,192,192]{3,2,1,0:T(8,128)} copy(f32[3,3,192,192]{3,2,1,0:T(8,128)S(1)} %bitcast.7) | data formatting | bytes 2654208
Async XLA Ops:
  0.6 1.2 %copy-start = (bf16[3,3,192,192]{3,2,1,0:T(8,128)(2,1)S(1)}, bf16[3,3,192,192]{3,2,1,0:T(8,128)(2,1)}, u32[]{:S(2)}) copy-start(bf16[3,3,192,192]{3,2,1,0:T(8,128)(2,1)} %param.5) | copy-start | bytes 1990660
  1.8 1.1 %copy-start.1 = (bf16[8,256,192]{1,2,0:T(8,128)(2,1)S(1)}, bf16[8,256,192]{1,2,0:T(8,128)(2,1)}, u32[]{:S(2)}) copy-start(bf16[8,256,192]{1,2,0:T(8,128)(2,1)} %param.4) | copy-start | bytes 2359300
  2.9 0.9 %copy-start.2 = (bf16[1,512,192]{1,2,0:T(8,128)(2,1)S(1)}, bf16[1,512,192]{1,2,0:T(8,128)(2,1)}, u32[]{:S(2)}) copy-start(bf16[1,512,192]{1,2,0:T(8,128)(2,1)} %param.3) | copy-start | bytes 589828

commit v2 on v1

--- a/solution.py
+++ b/solution.py
@@ -30,11 +30,11 @@
     return lax.broadcasted_iota(jnp.int32, shape, dim)
 
 
-def kernel(sizes, g_hbm, x_hbm, w_hbm, ig_hbm, fg_hbm, gsend, gcat, gshift, xin, w, xd, ig2, igo, terms, dbuf,
-           sbuf, rbuf, acc, zbuf, zfar, zown, fin, agbuf, fgo,
+def kernel(sizes, g_hbm, x_hbm, w_hbm, igo, agbuf, gsend, gcat, gshift, xin, w, xd, ig2, terms, dbuf,
+           sbuf, rbuf, acc, zbuf, zfar, zown, fin,
            load_sem, gs_sem, gr_sem, ds_sem, dr_sem, xs_sem, xr_sem, ns_sem, nr_sem, fs_sem, fr_sem,
-           as_sem, ar_sem, os_sem, or_sem, ps_sem, pr_sem, out_sem):
-    nyl, nx, nz, nyh, nzl, chunk, scale = sizes
+           as_sem, ar_sem, os_sem, or_sem, ps_sem, pr_sem):
+    nyl, nx, nz, nyh, nzl, chunk = sizes
     planes = nx * nyl * nyh
     nzh = nz // nzl
     piece = chunk // nzl
@@ -64,6 +64,7 @@
         px, py = (x + dx) % nx, (y + dy) % ny
         return px * ny + py, {X: px, YHI: py // nyl, YLO: py % nyl}
 
+    sent = []
     offsets = [(dx, dy) for dx in range(nx) for dy in range(ny) if (dx, dy) != (0, 0)]
     offsets.sort(key=lambda o: -(min(o[0], nx - o[0]) + min(o[1], ny - o[1])))
 
@@ -105,6 +106,32 @@
     def _():
         gcat[:, 512:640] = jnp.zeros((C + 16, 128), BF16)
 
+    @pl.when((col == 0) & (row > 0))
+    def _():
+        pl.semaphore_wait(barrier, met + 4)
+
+    @pl.when((col != 0) | (row == 0))
+    def _():
+        pl.semaphore_wait(barrier, met)
+
+    def g_copy(c, slot, where, sem):
+        return pltpu.make_async_remote_copy(
+            src_ref=gsend.at[:, pl.ds(pl.multiple_of(c * 128, 128), 128)],
+            dst_ref=gcat.at[:, pl.ds(pl.multiple_of(slot * 128, 128), 128)],
+            send_sem=gs_sem.at[sem], recv_sem=gr_sem.at[slot], device_id=where, device_id_type=MESH)
+
+    peers = [(col + d) % 4 for d in (2, 3, 1)]
+    for n, c in enumerate(peers):
+        copy = g_copy(c, col, at_col(c), n)
+        copy.start()
+        sent.append(copy)
+    upward = [g_copy(c, 4, at_row(row - 1) | at_col(c), 3 + c) for c in range(4)]
+
+    @pl.when((col == 0) & (row > 0))
+    def _():
+        for copy in upward:
+            copy.start()
+
     load_x.wait()
     r256, c256 = iota((256, 256), 0), iota((256, 256), 1)
     part = jnp.where(r256 == 2 * (c256 % 128) + c256 // 128, 1.0, 0.0).astype(BF16)
@@ -114,31 +141,6 @@
         lanes = slice(128 * (p // 2), 128 * (p // 2) + 128)
         xd[p % 2, 0, :, lanes] = both[:, 0:128]
         xd[p % 2, 1, :, lanes] = both[:, 128:256]
-
-    @pl.when((col == 0) & (row > 0))
-    def _():
-        pl.semaphore_wait(barrier, met + 4)
-
-    @pl.when((col != 0) | (row == 0))
-    def _():
-        pl.semaphore_wait(barrier, met)
-
-    def g_copy(c, slot, where, sem):
-        return pltpu.make_async_remote_copy(
-            src_ref=gsend.at[:, pl.ds(pl.multiple_of(c * 128, 128), 128)],
-            dst_ref=gcat.at[:, pl.ds(pl.multiple_of(slot * 128, 128), 128)],
-            send_sem=gs_sem.at[sem], recv_sem=gr_sem.at[slot], device_id=where, device_id_type=MESH)
-
-    peers = [(col + d) % 4 for d in (2, 3, 1)]
-    g_sent = [g_copy(c, col, at_col(c), n) for n, c in enumerate(peers)]
-    for copy in g_sent:
-        copy.start()
-    upward = [g_copy(c, 4, at_row(row - 1) | at_col(c), 3 + c) for c in range(4)]
-
-    @pl.when((col == 0) & (row > 0))
-    def _():
-        for copy in upward:
-            copy.start()
 
     for d in (1, 2, 3):
         g_copy(0, (col + d) % 4, at_col(0), 0).wait_recv()
@@ -189,6 +191,7 @@
         src_ref=terms.at[1 - core], dst_ref=dbuf, send_sem=ds_sem, recv_sem=dr_sem,
         device_id={CORE: 1 - core}, device_id_type=MESH)
     pair.start()
+    sent.append(pair)
     pair.wait_recv()
 
     def plane_copy(n, source, slot, where):
@@ -196,14 +199,13 @@
             src_ref=sbuf.at[source], dst_ref=rbuf.at[slot], send_sem=xs_sem.at[n], recv_sem=xr_sem.at[slot],
             device_id=where, device_id_type=MESH)
 
-    plane_sent = []
     for n, (dx, dy) in enumerate(offsets):
         q, where = at_plane(dx, dy)
         at = pl.ds(pl.multiple_of(q * chunk, chunk), chunk)
         sbuf[q] = (terms[core, at, :] + dbuf[at, :]).astype(BF16)
         copy = plane_copy(n, q, me, where)
         copy.start()
-        plane_sent.append(copy)
+        sent.append(copy)
     at = pl.ds(pl.multiple_of(me * chunk, chunk), chunk)
     acc[...] = terms[core, at, :] + dbuf[at, :]
 
@@ -232,8 +234,6 @@
             ig2[row_par, i, :, 128 * col_par : 128 * col_par + 128] = placed[:, 128 * i : 128 * i + 128]
     for p in range(8):
         igo[p] = dot_nn(ig2[p % 2, p // 2], join).astype(BF16)
-    store_ig = pltpu.make_async_copy(igo, ig_hbm, out_sem.at[0])
-    store_ig.start()
 
     total = acc[...]
     for dx, dy in reversed(offsets):
@@ -247,12 +247,11 @@
             src_ref=acc.at[pl.ds(pl.multiple_of(k * piece, 8), piece)], dst_ref=zbuf.at[slot],
             send_sem=ns_sem.at[n], recv_sem=nr_sem.at[slot], device_id={Z: where}, device_id_type=MESH)
 
-    near_sent = []
     for d in range(1, nzl):
         k = (zl + d) % nzl
         copy = near_copy(d - 1, k, zl, zh * nzl + k)
         copy.start()
-        near_sent.append(copy)
+        sent.append(copy)
     total = acc[pl.ds(pl.multiple_of(zl * piece, 8), piece)]
     for d in range(1, nzl):
         k = (zl + d) % nzl
@@ -266,11 +265,10 @@
             src_ref=zown, dst_ref=zfar.at[slot], send_sem=fs_sem.at[n], recv_sem=fr_sem.at[slot],
             device_id={Z: where}, device_id_type=MESH)
 
-    far_sent = []
     for n, d in enumerate(sorted(range(1, nzh), key=lambda d: -min(d, nzh - d))):
         copy = far_copy(n, zh, ((zh + d) % nzh) * nzl + zl)
         copy.start()
-        far_sent.append(copy)
+        sent.append(copy)
     for d in range(1, nzh):
         far_copy(0, (zh + d) % nzh, z).wait_recv()
     total = zfar[0]
@@ -285,11 +283,10 @@
             src_ref=fin.at[part_of], dst_ref=fin.at[part_of], send_sem=as_sem.at[n], recv_sem=ar_sem.at[k],
             device_id={Z: where}, device_id_type=MESH)
 
-    gather_sent = []
     for d in range(1, nzl):
         copy = gather_copy(d - 1, zl, zh * nzl + (zl + d) % nzl)
         copy.start()
-        gather_sent.append(copy)
+        sent.append(copy)
     for d in range(1, nzl):
         gather_copy(0, (zl + d) % nzl, z).wait_recv()
 
@@ -307,21 +304,34 @@
             device_id={CORE: 1 - core}, device_id_type=MESH)
 
     agbuf[core, pl.ds(pl.multiple_of(me * chunk, chunk), chunk)] = fin[...].astype(BF16)
-    spread_sent = []
     for n, (dx, dy) in enumerate(offsets):
         copy = spread_copy(n, me, at_plane(dx, dy)[1])
         copy.start()
-        spread_sent.append(copy)
-    pass_sent = [pass_copy(me, core)]
-    pass_sent[0].start()
+        sent.append(copy)
+    copy = pass_copy(me, core)
+    copy.start()
+    sent.append(copy)
     for dx, dy in reversed(offsets):
         q = at_plane(dx, dy)[0]
         spread_copy(0, q, {}).wait_recv()
         copy = pass_copy(q, core)
         copy.start()
-        pass_sent.append(copy)
+        sent.append(copy)
     for q in range(planes):
         pass_copy(q, 1 - core).wait_recv()
+
+    for copy in sent:
+        copy.wait_send()
+
+    @pl.when((col == 0) & (row > 0))
+    def _():
+        for copy in upward:
+            copy.wait_send()
+
+
+def finish(scale, igo, agbuf, ig_hbm, fg_hbm, fgo, sem):
+    store_ig = pltpu.make_async_copy(igo, ig_hbm, sem.at[9])
+    store_ig.start()
 
     def packed(begin, count):
         cut = min(max(HALF - begin, 0), count)
@@ -333,25 +343,19 @@
         values = parts[0] if len(parts) == 1 else jnp.concatenate(parts, axis=0)
         return values.astype(F32) * scale
 
+    stores = []
     for t in range(9):
         start = TAP_ROWS * t
         fgo[t, :, 0:128] = packed(start, C)
         rest = packed(start + C, C // 2)
         fgo[t, 0 : C // 2, 128:C] = rest[:, 0:64]
         fgo[t, C // 2 : C, 128:C] = pltpu.roll(rest, 64, 1)[:, 0:64]
-    store_fg = pltpu.make_async_copy(fgo, fg_hbm, out_sem.at[1])
-    store_fg.start()
-
-    for copy in g_sent + [pair] + plane_sent + near_sent + far_sent + gather_sent + spread_sent + pass_sent:
-        copy.wait_send()
-
-    @pl.when((col == 0) & (row > 0))
-    def _():
-        for copy in upward:
-            copy.wait_send()
-
+        store = pltpu.make_async_copy(fgo.at[t], fg_hbm.at[t], sem.at[t])
+        store.start()
+        stores.append(store)
+    for store in stores:
+        store.wait()
     store_ig.wait()
-    store_fg.wait()
 
 
 def near_size(nz):
@@ -367,20 +371,18 @@
     g = jnp.transpose(grad_out, (0, 2, 1)).reshape(C, grad_out.shape[1])
     xt = jnp.transpose(inputs, (0, 2, 1))
     wt = weight.reshape(9, C, C)
-    sizes = (nyl, nx, nz, nyh, nzl, chunk, scale)
+    sizes = (nyl, nx, nz, nyh, nzl, chunk)
     dma = pltpu.SemaphoreType.DMA
     hbm = pl.BlockSpec(memory_space=pl.ANY)
     n = planes - 1
     nzh = nz // nzl
     piece = chunk // nzl
-    ig, fg = pl.pallas_call(
+    vmem = pl.BlockSpec(memory_space=pltpu.VMEM)
+    igo, agbuf = pl.pallas_call(
         functools.partial(kernel, sizes),
-        out_shape=(
-            jax.ShapeDtypeStruct(xt.shape, BF16),
-            jax.ShapeDtypeStruct((9, C, C), F32),
-        ),
+        out_shape=(pltpu.VMEM(xt.shape, BF16), pltpu.VMEM((2, planes * chunk, 128), BF16)),
         in_specs=[hbm] * 3,
-        out_specs=(hbm, hbm),
+        out_specs=(vmem, vmem),
         scratch_shapes=[
             pltpu.VMEM((C + 16, 512), BF16),
             pltpu.VMEM((C + 16, 640), BF16),
@@ -389,7 +391,6 @@
             pltpu.VMEM((9, C, C), BF16),
             pltpu.VMEM((2, 2, C, 512), BF16),
             pltpu.VMEM((2, 4, C, 256), BF16),
-            pltpu.VMEM(xt.shape, BF16),
             pltpu.VMEM((2, planes * chunk, 128), F32),
             pltpu.VMEM((planes * chunk, 128), F32),
             pltpu.VMEM((planes, chunk, 128), BF16),
@@ -399,16 +400,22 @@
             pltpu.VMEM((nzh, piece, 128), F32),
             pltpu.VMEM((piece, 128), F32),
             pltpu.VMEM((chunk, 128), F32),
-            pltpu.VMEM((2, planes * chunk, 128), BF16),
-            pltpu.VMEM((9, C, C), F32),
             dma((3,)), dma((7,)), dma((5,)), dma, dma, dma((n,)), dma((planes,)),
             dma((nzl,)), dma((nzl,)), dma((nzh,)), dma((nzh,)), dma((nzl,)), dma((nzl,)),
-            dma((n,)), dma((planes,)), dma((planes,)), dma((planes,)), dma((2,)),
+            dma((n,)), dma((planes,)), dma((planes,)), dma((planes,)),
         ],
         compiler_params=pltpu.CompilerParams(
-            collective_id=0, has_side_effects=True, vmem_limit_bytes=48 * 1024 * 1024
+            collective_id=0, has_side_effects=True, vmem_limit_bytes=65400000
         ),
     )(g, xt, wt)
+    ig, fg = pl.pallas_call(
+        functools.partial(finish, scale),
+        out_shape=(jax.ShapeDtypeStruct(xt.shape, BF16), jax.ShapeDtypeStruct((9, C, C), F32)),
+        in_specs=[vmem, vmem],
+        out_specs=(hbm, hbm),
+        scratch_shapes=[pltpu.VMEM((9, C, C), F32), dma((10,))],
+        compiler_params=pltpu.CompilerParams(vmem_limit_bytes=16 * 1024 * 1024),
+    )(igo, agbuf)
     return jnp.transpose(ig, (0, 2, 1)), fg.reshape(3, 3, C, C)
 
 

time: 62.5 us -> 57.4 us (0.918)
  local copies, waits for them, and re-layouts: 5.31 us -> 0 us
    unnamed x8 -> x0, local copies, waits for them, and re-layouts: 5.31 us -> none
    pallas_call x1 -> x2, Pallas kernels: 56.3 us -> 56.6 us  [the longest x1 55.1 us: per_device(): pl.pallas_call(functools.partial(kernel, sizes), out_shape=(pltpu.VMEM(xt...]
where the time goes in v2:
time: 57.4 us; the launch traced here: 57.3 us
  Pallas kernels  56.6 us (99%)
  between operations  0.64 us (1%)
    pallas_call x1, Pallas kernels, per_device(): pl.pallas_call(functools.partial(kernel, sizes), out_shape=(pltpu.VMEM(xt...  55.1 us
    pallas_call x1, Pallas kernels, per_device(): pl.pallas_call(functools.partial(finish, scale), out_shape=(jax.ShapeDtyp...  1.54 us

profile of v2, /device:TPU:1, one launch (start us, length us, event | category | flops | bytes accessed | tf_op | source)
XLA Modules:
  0.0 57.3 jit_solution(14523387320150288787)
XLA Ops:
  0.6 55.1 %shard_map.50 = (bf16[8,192,256]{2,1,0:T(8,128)(2,1)S(1)}, bf16[2,1536,128]{2,1,0:T(8,128)(2,1)S(1)}) custom-call(bf16[192,512]{1,0:T(8,128)(2,1)} %bitcast.9, bf16[8,192,256]{2,1,0:T(8,128)(2,1)} %bitcast.8, bf16[9,192,192]{2,1,0:T(8,128)(2,1)} %bitcast.7), custom_call_target="tpu_custom_call" | custom-call | tf_op jit(solution)/shard_map/pallas_call | solution.py:381
  55.7 1.5 %shard_map.51 = (bf16[8,192,256]{2,1,0:T(8,128)(2,1)}, f32[9,192,192]{2,1,0:T(8,128)}) custom-call(bf16[8,192,256]{2,1,0:T(8,128)(2,1)S(1)} %get-tuple-element.6.igo, bf16[2,1536,128]{2,1,0:T(8,128)(2,1)S(1)} %get-tuple-element.7.agbuf), custom_call_target="tpu_custom_call" | custom-call | tf_op jit(solution)/shard_map/pallas_call | solution.py:411
